TPU v7x, 32 devices: a whole 2x2x4 slice. The times are simulated.
32 devices in a mesh: section: 2 (over x), expert: 16 (over z, y, core).
Axes of the slice: x: 2, y: 2, z: 4, core: 2. Of those that a mesh axis runs over, the one named last changes fastest.
Arguments:
- images: bfloat16 [32, 256, 1408], P(('section', 'expert')), may hold values from -6 to 6
- norm_gain: bfloat16 [1408], replicated, may hold values from 0.5 to 1.5
- slot_map: bfloat16 [1408, 16], replicated, may hold values from -0.15625 to 0.15625
- logit_scale: float32 [1], replicated, may hold values from 30 to 80
- up_weight: bfloat16 [16, 5120, 1408], P('expert', 'section'), may hold values from -0.625 to 0.625
- down_weight: bfloat16 [16, 5120, 1408], P('expert', 'section'), may hold values from -0.3125 to 0.3125
Outputs:
- block_out: bfloat16 [32, 256, 1408], P(('section', 'expert'))
All inputs are finite; a program needn't handle non-finite values.
Results may differ from a plain program's by a relative error of at most 0.011.
Values may be sent and summed in bfloat16 or wider, within the bound.
A program may use at most 64 MiB of HBM per device.

v0:
```python
import jax
import jax.numpy as jnp
from jax import lax
from jax.sharding import PartitionSpec as P

epsilon = 1e-06


def normalize(inputs, gain_row):
    values = inputs.astype(jnp.float32)
    spread = jnp.mean(values * values, axis=-1, keepdims=True)
    return (values * lax.rsqrt(spread + epsilon) * gain_row.astype(jnp.float32)).astype(
        jnp.bfloat16
    )


def weights_from(raw, normed, slot_cols, scale_now):
    values = normed.astype(jnp.float32)
    token_norm = jnp.sqrt(jnp.sum(values * values, axis=-1) + epsilon)
    columns = slot_cols.astype(jnp.float32)
    column_norm = jnp.sqrt(jnp.sum(columns * columns, axis=0) + epsilon)
    logits = scale_now * raw / (token_norm[:, None, :] * column_norm[None, :, None])
    scores = jnp.exp(logits)
    dispatch = (scores / jnp.sum(scores, axis=-1, keepdims=True)).astype(jnp.bfloat16)
    combine = (scores / jnp.sum(scores, axis=1, keepdims=True)).astype(jnp.bfloat16)
    return (dispatch, combine)


def local(images, norm_gain, slot_map, logit_scale, up_weight, down_weight):
    position = lax.axis_index("section")
    normed = normalize(images, norm_gain)
    raw = jnp.einsum("itd,de->iet", normed, slot_map, preferred_element_type=jnp.float32)
    dispatch, combine = weights_from(raw, normed, slot_map, logit_scale[0])
    slot_in = jnp.einsum(
        "iet,itd->eid", dispatch, normed, preferred_element_type=jnp.float32
    ).astype(jnp.bfloat16)
    slots = lax.all_to_all(slot_in, "expert", split_axis=0, concat_axis=1, tiled=True)
    count = slots.shape[1]
    gathered = lax.all_gather(slots, "section", axis=1, tiled=True)
    hidden = jax.nn.gelu(
        jnp.einsum("esd,efd->esf", gathered, up_weight, preferred_element_type=jnp.float32)
    ).astype(jnp.bfloat16)
    partial_sum = jnp.einsum(
        "esf,efd->esd", hidden, down_weight, preferred_element_type=jnp.float32
    )
    totals = lax.psum(partial_sum, "section")
    own_rows = lax.dynamic_slice_in_dim(totals, position * count, count, 1)
    result = own_rows.astype(jnp.bfloat16)
    back = lax.all_to_all(result, "expert", split_axis=1, concat_axis=0, tiled=True)
    mixed = jnp.einsum("iet,eid->itd", combine, back, preferred_element_type=jnp.float32)
    return (images.astype(jnp.float32) + mixed).astype(jnp.bfloat16)


def solution(mesh):
    return jax.shard_map(
        local,
        mesh=mesh,
        in_specs=(
            P(("section", "expert"), None, None),
            P(),
            P(),
            P(),
            P("expert", "section", None),
            P("expert", "section", None),
        ),
        out_specs=P(("section", "expert"), None, None),
        check_vma=False,
    )
```

profile of v0, /device:TPU:0, one launch (start us, length us, event | category | flops | bytes accessed | tf_op | source)
XLA Modules:
  0.0 58.3 jit_solution(4352403339752684257)
XLA Ops:
  0.0 0.0 copy-start.1
  0.0 0.0 copy-start
  0.7 0.9 %multiply_reduce_fusion.1 = f32[16]{0:T(128)S(1)} fusion(bf16[1408,16]{0,1:T(8,128)(2,1)} %param.8), kind=kLoop, calls=%fused_computation.37 | loop fusion | flops 67568 | bytes 45120 | tf_op jit(solution)/shard_map/reduce_sum | solution.py:21
  1.6 1.3 %fusion.10 = f32[256]{0:T(256)S(1)} fusion(bf16[1,256,1408]{2,1,0:T(8,128)(2,1)} %param.6), kind=kLoop, calls=%fused_computation.12 | loop fusion | flops 1081088 | bytes 721920 | tf_op jit(solution)/shard_map/reduce_sum | solution.py:11
  3.0 0.7 %convert_element_type.44 = f32[1408]{0:T(1024)S(1)} convert(bf16[1408]{0:T(1024)(128)(2,1)} %param.7) | non-fusion elementwise | flops 1408 | bytes 8448 | tf_op jit(solution)/shard_map/convert_element_type | solution.py:12
  3.7 1.5 %multiply_reduce_fusion = f32[256]{0:T(256)S(1)} fusion(f32[1408]{0:T(1024)S(1)} %convert_element_type.44, f32[256]{0:T(256)S(1)} %add_rsqrt_fusion, bf16[1,256,1408]{2,1,0:T(8,128)(2,1)} %param.6), kind=kLoop, calls=%fused_computation.15 | loop fusion | flops 2522880 | bytes 728576 | tf_op jit(solution)/shard_map/reduce_sum | solution.py:19
  5.2 0.0 copy-done.1
  5.2 0.0 copy-done
  5.2 0.5 fusion.48
  5.7 0.4 fusion.9
  6.1 0.6 %broadcast.46 = bf16[]{:T(256)} broadcast(bf16[]{:T(256)} %constant.65), dimensions={} | broadcast | bytes 4 | tf_op jit(solution)/shard_map/convert_element_type | solution.py:36
  6.7 0.7 %reduce.6 = bf16[16,1408]{1,0:T(8,128)(2,1)S(1)} reduce(bf16[16,1,1408]{2,0,1:T(8,128)(2,1)S(1)} %fusion.9, bf16[]{:T(256)} %broadcast.46), dimensions={1}, to_apply=%copy.9.reduce_sub_computation | reduce | bytes 90114 | tf_op jit(solution)/shard_map/convert_element_type | solution.py:36
  7.4 0.7 %reshape.104 = bf16[16,2,704]{2,1,0:T(2,128)(2,1)} reshape(bf16[16,1408]{1,0:T(8,128)(2,1)S(1)} %reduce.6) | data formatting | bytes 90112
  8.1 7.4 %all-to-all-start = ((bf16[16,2,704]{2,1,0:T(2,128)(2,1)}), bf16[16,2,704]{2,1,0:T(2,128)(2,1)S(1)}, u32[]{:S(2)}, u32[]{:S(2)}) async-start(bf16[16,2,704]{2,1,0:T(2,128)(2,1)} %reshape.104), calls=%async_computation | async-start | bytes 98304 | tf_op jit(solution)/shard_map/all_to_all | solution.py:37
  15.5 6.8 %all-to-all-done = bf16[16,2,704]{2,1,0:T(2,128)(2,1)S(1)} async-done(((bf16[16,2,704]{2,1,0:T(2,128)(2,1)}), bf16[16,2,704]{2,1,0:T(2,128)(2,1)S(1)}, u32[]{:S(2)}, u32[]{:S(2)}) %all-to-all-start) | async-done | bytes 45088 | tf_op jit(solution)/shard_map/all_to_all | solution.py:37
  22.3 0.1 reshape.105
  22.4 4.7 %all-gather = bf16[32,1,1408]{2,0,1:T(8,128)(2,1)S(1)} all-gather(bf16[16,1,1408]{2,0,1:T(8,128)(2,1)S(1)} %copy.10), channel_id=2, replica_groups=mesh['section'=2,'expert'=16] {'section'}, dimensions={0}, use_global_device_ids=true | all-gather | bytes 135168 | tf_op jit(solution)/shard_map/all_gather | solution.py:39
  27.2 8.4 %fusion.6 = f32[1,32,1408]{2,1,0:T(8,128)S(1)} fusion(bf16[1,2560,1408]{2,1,0:T(8,128)(2,1)} %param.11, bf16[1,2560,1408]{2,1,0:T(8,128)(2,1)} %param.10, bf16[32,1,1408]{2,0,1:T(8,128)(2,1)S(1)} %all-gather), kind=kOutput, calls=%fused_computation.7 | convolution fusion | flops 462110720 | bytes 14688256 | tf_op jit(solution)/shard_map/esf,efd->esd/dot_general | solution.py:43
  35.6 10.9 %all-reduce.1 = bf16[1,32,1408]{2,1,0:T(8,128)(2,1)S(1)} all-reduce(f32[1,32,1408]{2,1,0:T(8,128)S(1)} %fusion.6), channel_id=1, replica_groups=mesh['section'=2,'expert'=16] {'section'}, use_global_device_ids=true, to_apply=%region_5.0 | all-reduce | flops 45056 | bytes 270336 | tf_op jit(solution)/shard_map/psum | solution.py:46
  46.5 0.1 copy.18
  46.6 0.9 %reduce.7 = bf16[16,1408]{1,0:T(8,128)(2,1)S(1)} reduce(bf16[16,1,1408]{2,1,0:T(2,128)(2,1)S(1)} %bitcast.53, bf16[]{:T(256)} %broadcast.46), dimensions={1}, to_apply=%bitcast.51.reduce_sub_computation | reduce | bytes 90114
  47.5 0.1 reshape.106
  47.6 9.3 %all_to_all.21 = bf16[16,2,704]{2,1,0:T(2,128)(2,1)S(1)} all-to-all(bf16[16,2,704]{2,1,0:T(2,128)(2,1)S(1)} %reshape.106), channel_id=1, replica_groups=mesh['section'=2,'expert'=16] {'expert'}, dimensions={0} | all-to-all | bytes 90112 | tf_op jit(solution)/shard_map/all_to_all | solution.py:49
  57.0 0.1 reshape.107
  57.1 1.3 %fusion.5 = bf16[1,256,1408]{2,1,0:T(8,128)(2,1)} fusion(bf16[1,256,1408]{2,1,0:T(8,128)(2,1)S(1)} %copy-done, bf16[1,16,1408]{2,0,1:T(2,128)(2,1)S(1)} %bitcast.54, f32[16,256]{1,0:T(8,128)S(1)} %get-tuple-element.7, f32[256]{0:T(256)S(1)} %get-tuple-element.5), kind=kOutput, calls=%fused_computation.6 | convolution fusion | flops 12623872 | bytes 1504256 | tf_op jit(solution)/shard_map/iet,eid->itd/dot_general | solution.py:50
  (5 shorter events, 0.1 us)
Async XLA Ops:
  0.0 5.2 %copy-start.1 = (bf16[1408,16]{0,1:T(8,128)(2,1)S(1)}, bf16[1408,16]{0,1:T(8,128)(2,1)}, u32[]{:S(2)}) copy-start(bf16[1408,16]{0,1:T(8,128)(2,1)} %param.8) | copy-start | bytes 135172
  0.0 5.2 %copy-start = (bf16[1,256,1408]{2,1,0:T(8,128)(2,1)S(1)}, bf16[1,256,1408]{2,1,0:T(8,128)(2,1)}, u32[]{:S(2)}) copy-start(bf16[1,256,1408]{2,1,0:T(8,128)(2,1)} %param.6) | copy-start | bytes 2162692
  8.1 14.2 %all-to-all-start = ((bf16[16,2,704]{2,1,0:T(2,128)(2,1)}), bf16[16,2,704]{2,1,0:T(2,128)(2,1)S(1)}, u32[]{:S(2)}, u32[]{:S(2)}) async-start(bf16[16,2,704]{2,1,0:T(2,128)(2,1)} %reshape.104), calls=%async_computation | async-start | bytes 98304 | tf_op jit(solution)/shard_map/all_to_all | solution.py:37
where the time goes:
time: 58.8 us; the launch traced here: 58.3 us
  blocking collectives  24.9 us (42%)
  matrix products  10.6 us (18%)
  starting transfers between devices  7.41 us (13%)
  waiting for transfers between devices  6.76 us (11%)
  other arithmetic  6.08 us (10%)
  local copies, waits for them, and re-layouts  1.79 us (3%)
  between operations  0.82 us (1%)
    psum x1, blocking collectives, local(): totals = lax.psum(partial_sum, 'section')  10.9 us
    all_to_all x1, blocking collectives, local(): lax.all_to_all(result, 'expert', split_axis=1, concat_axis=0, tiled=True)  9.34 us
    dot_general x1, matrix products, local(): jnp.einsum('esf,efd->esd', hidden, down_weight, preferred_element_type=jn...  8.44 us
    all_to_all x1, starting transfers between devices, local(): lax.all_to_all(slot_in, 'expert', split_axis=0, concat_axis=1, tiled=True)  7.41 us
    all_to_all x1, waiting for transfers between devices, local(): lax.all_to_all(slot_in, 'expert', split_axis=0, concat_axis=1, tiled=True)  6.76 us
    all_gather x1, blocking collectives, local(): gathered = lax.all_gather(slots, 'section', axis=1, tiled=True)  4.71 us
    reduce_sum x1, other arithmetic, weights_from(): token_norm = jnp.sqrt(jnp.sum(values * values, axis=-1) + epsilon)  1.48 us
    reduce_sum x1, other arithmetic, normalize(): spread = jnp.mean(values * values, axis=-1, keepdims=True)  1.34 us
  transfers between devices with their start and end apart: 1, of which 1 were waited for; matrix products, arithmetic and copies ran while one was open for 0% of the time, Pallas kernels for 0%

commit v1 on v0

--- a/solution.py
+++ b/solution.py
@@ -2,6 +2,7 @@
 import jax.numpy as jnp
 from jax import lax
 from jax.sharding import PartitionSpec as P
+from jax.lax import all_gather
 
 epsilon = 1e-06
 
@@ -43,7 +44,7 @@
     partial_sum = jnp.einsum(
         "esf,efd->esd", hidden, down_weight, preferred_element_type=jnp.float32
     )
-    totals = lax.psum(partial_sum, "section")
+    totals = jnp.sum(all_gather(partial_sum, "section"), 0)
     own_rows = lax.dynamic_slice_in_dim(totals, position * count, count, 1)
     result = own_rows.astype(jnp.bfloat16)
     back = lax.all_to_all(result, "expert", split_axis=1, concat_axis=0, tiled=True)

time: 58.8 us -> 54.1 us (0.920)
  blocking collectives: 24.9 us -> 20.2 us
    psum x1 -> x0, blocking collectives: 10.9 us -> none  [local(): totals = lax.psum(partial_sum, 'section')]
    all_gather x0 -> x1, blocking collectives: none -> 6.17 us  [local(): totals = jnp.sum(all_gather(partial_sum, 'section'), 0)]
where the time goes in v1:
time: 54.1 us; the launch traced here: 53.7 us
  blocking collectives  20.2 us (37%)
  matrix products  10.6 us (20%)
  starting transfers between devices  7.41 us (14%)
  waiting for transfers between devices  6.76 us (12%)
  other arithmetic  6.1 us (11%)
  local copies, waits for them, and re-layouts  1.79 us (3%)
  between operations  0.81 us (1%)
    all_to_all x1, blocking collectives, local(): lax.all_to_all(result, 'expert', split_axis=1, concat_axis=0, tiled=True)  9.34 us
    dot_general x1, matrix products, local(): jnp.einsum('esf,efd->esd', hidden, down_weight, preferred_element_type=jn...  8.44 us
    all_to_all x1, starting transfers between devices, local(): lax.all_to_all(slot_in, 'expert', split_axis=0, concat_axis=1, tiled=True)  7.41 us
    all_to_all x1, waiting for transfers between devices, local(): lax.all_to_all(slot_in, 'expert', split_axis=0, concat_axis=1, tiled=True)  6.76 us
    all_gather x1, blocking collectives, local(): totals = jnp.sum(all_gather(partial_sum, 'section'), 0)  6.17 us
    all_gather x1, blocking collectives, local(): gathered = lax.all_gather(slots, 'section', axis=1, tiled=True)  4.71 us
    reduce_sum x1, other arithmetic, weights_from(): token_norm = jnp.sqrt(jnp.sum(values * values, axis=-1) + epsilon)  1.48 us
    reduce_sum x1, other arithmetic, normalize(): spread = jnp.mean(values * values, axis=-1, keepdims=True)  1.34 us
  transfers between devices with their start and end apart: 1, of which 1 were waited for; matrix products, arithmetic and copies ran while one was open for 0% of the time, Pallas kernels for 0%

profile of v1, /device:TPU:0, one launch (start us, length us, event | category | flops | bytes accessed | tf_op | source)
XLA Modules:
  0.0 53.7 jit_solution(17233985536007423341)
XLA Ops:
  0.0 0.0 copy-start.1
  0.0 0.0 copy-start
  0.7 0.9 %multiply_reduce_fusion.1 = f32[16]{0:T(128)S(1)} fusion(bf16[1408,16]{0,1:T(8,128)(2,1)} %param.8), kind=kLoop, calls=%fused_computation.36 | loop fusion | flops 67568 | bytes 45120 | tf_op jit(solution)/shard_map/reduce_sum | solution.py:22
  1.6 1.3 %fusion.7 = f32[256]{0:T(256)S(1)} fusion(bf16[1,256,1408]{2,1,0:T(8,128)(2,1)} %param.6), kind=kLoop, calls=%fused_computation.11 | loop fusion | flops 1081088 | bytes 721920 | tf_op jit(solution)/shard_map/reduce_sum | solution.py:12
  3.0 0.7 %convert_element_type.47 = f32[1408]{0:T(1024)S(1)} convert(bf16[1408]{0:T(1024)(128)(2,1)} %param.7) | non-fusion elementwise | flops 1408 | bytes 8448 | tf_op jit(solution)/shard_map/convert_element_type | solution.py:13
  3.7 1.5 %multiply_reduce_fusion = f32[256]{0:T(256)S(1)} fusion(f32[1408]{0:T(1024)S(1)} %convert_element_type.47, f32[256]{0:T(256)S(1)} %add_rsqrt_fusion, bf16[1,256,1408]{2,1,0:T(8,128)(2,1)} %param.6), kind=kLoop, calls=%fused_computation.14 | loop fusion | flops 2522880 | bytes 728576 | tf_op jit(solution)/shard_map/reduce_sum | solution.py:20
  5.2 0.0 copy-done.1
  5.2 0.0 copy-done
  5.2 0.5 fusion.46
  5.7 0.4 fusion.6
  6.1 0.6 %broadcast.46 = bf16[]{:T(256)} broadcast(bf16[]{:T(256)} %constant.65), dimensions={} | broadcast | bytes 4 | tf_op jit(solution)/shard_map/convert_element_type | solution.py:37
  6.7 0.7 %reduce.8 = bf16[16,1408]{1,0:T(8,128)(2,1)S(1)} reduce(bf16[16,1,1408]{2,0,1:T(8,128)(2,1)S(1)} %fusion.6, bf16[]{:T(256)} %broadcast.46), dimensions={1}, to_apply=%copy.8.reduce_sub_computation | reduce | bytes 90114 | tf_op jit(solution)/shard_map/convert_element_type | solution.py:37
  7.4 0.7 %reshape.110 = bf16[16,2,704]{2,1,0:T(2,128)(2,1)} reshape(bf16[16,1408]{1,0:T(8,128)(2,1)S(1)} %reduce.8) | data formatting | bytes 90112
  8.1 7.4 %all-to-all-start = ((bf16[16,2,704]{2,1,0:T(2,128)(2,1)}), bf16[16,2,704]{2,1,0:T(2,128)(2,1)S(1)}, u32[]{:S(2)}, u32[]{:S(2)}) async-start(bf16[16,2,704]{2,1,0:T(2,128)(2,1)} %reshape.110), calls=%async_computation | async-start | bytes 98304 | tf_op jit(solution)/shard_map/all_to_all | solution.py:38
  15.5 6.8 %all-to-all-done = bf16[16,2,704]{2,1,0:T(2,128)(2,1)S(1)} async-done(((bf16[16,2,704]{2,1,0:T(2,128)(2,1)}), bf16[16,2,704]{2,1,0:T(2,128)(2,1)S(1)}, u32[]{:S(2)}, u32[]{:S(2)}) %all-to-all-start) | async-done | bytes 45088 | tf_op jit(solution)/shard_map/all_to_all | solution.py:38
  22.3 0.1 reshape.111
  22.4 4.7 %all-gather = bf16[32,1,1408]{2,0,1:T(8,128)(2,1)S(1)} all-gather(bf16[16,1,1408]{2,0,1:T(8,128)(2,1)S(1)} %copy.9), channel_id=2, replica_groups=mesh['section'=2,'expert'=16] {'section'}, dimensions={0}, use_global_device_ids=true | all-gather | bytes 135168 | tf_op jit(solution)/shard_map/all_gather | solution.py:40
  27.2 8.4 %fusion = f32[32,1408]{1,0:T(8,128)S(1)} fusion(bf16[1,2560,1408]{2,1,0:T(8,128)(2,1)} %param.11, bf16[1,2560,1408]{2,1,0:T(8,128)(2,1)} %param.10, bf16[32,1,1408]{2,0,1:T(8,128)(2,1)S(1)} %all-gather), kind=kOutput, calls=%fused_computation | convolution fusion | flops 462110720 | bytes 14688256 | tf_op jit(solution)/shard_map/esf,efd->esd/dot_general | solution.py:44
  35.6 6.2 %all-gather.1 = f32[64,1408]{1,0:T(8,128)S(1)} all-gather(f32[32,1408]{1,0:T(8,128)S(1)} %fusion), channel_id=3, replica_groups=mesh['section'=2,'expert'=16] {'section'}, dimensions={0}, use_global_device_ids=true | all-gather | bytes 540672 | tf_op jit(solution)/shard_map/all_gather | solution.py:47
  41.8 0.1 copy.17
  41.9 0.9 %reduce.9 = bf16[16,1408]{1,0:T(8,128)(2,1)S(1)} reduce(bf16[16,1,1408]{2,1,0:T(2,128)(2,1)S(1)} %bitcast.53, bf16[]{:T(256)} %broadcast.46), dimensions={1}, to_apply=%bitcast.50.reduce_sub_computation | reduce | bytes 90114
  42.8 0.1 reshape.112
  42.9 9.3 %all_to_all.21 = bf16[16,2,704]{2,1,0:T(2,128)(2,1)S(1)} all-to-all(bf16[16,2,704]{2,1,0:T(2,128)(2,1)S(1)} %reshape.112), channel_id=1, replica_groups=mesh['section'=2,'expert'=16] {'expert'}, dimensions={0} | all-to-all | bytes 90112 | tf_op jit(solution)/shard_map/all_to_all | solution.py:50
  52.3 0.1 reshape.113
  52.4 1.3 %fusion.5 = bf16[1,256,1408]{2,1,0:T(8,128)(2,1)} fusion(bf16[1,256,1408]{2,1,0:T(8,128)(2,1)S(1)} %copy-done, bf16[1,16,1408]{2,0,1:T(2,128)(2,1)S(1)} %bitcast.54, f32[16,256]{1,0:T(8,128)S(1)} %get-tuple-element.7, f32[256]{0:T(256)S(1)} %get-tuple-element.5), kind=kOutput, calls=%fused_computation.6 | convolution fusion | flops 12623872 | bytes 1504256 | tf_op jit(solution)/shard_map/iet,eid->itd/dot_general | solution.py:51
  (6 shorter events, 0.1 us)
Async XLA Ops:
  0.0 5.2 %copy-start.1 = (bf16[1408,16]{0,1:T(8,128)(2,1)S(1)}, bf16[1408,16]{0,1:T(8,128)(2,1)}, u32[]{:S(2)}) copy-start(bf16[1408,16]{0,1:T(8,128)(2,1)} %param.8) | copy-start | bytes 135172
  0.0 5.2 %copy-start = (bf16[1,256,1408]{2,1,0:T(8,128)(2,1)S(1)}, bf16[1,256,1408]{2,1,0:T(8,128)(2,1)}, u32[]{:S(2)}) copy-start(bf16[1,256,1408]{2,1,0:T(8,128)(2,1)} %param.6) | copy-start | bytes 2162692
  8.1 14.2 %all-to-all-start = ((bf16[16,2,704]{2,1,0:T(2,128)(2,1)}), bf16[16,2,704]{2,1,0:T(2,128)(2,1)S(1)}, u32[]{:S(2)}, u32[]{:S(2)}) async-start(bf16[16,2,704]{2,1,0:T(2,128)(2,1)} %reshape.110), calls=%async_computation | async-start | bytes 98304 | tf_op jit(solution)/shard_map/all_to_all | solution.py:38
